TPU v7x, 32 devices: a whole 2x2x4 slice. The times are simulated.
32 devices in a mesh: dp: 16 (over z, y, core), mp: 2 (over x).
Axes of the slice: x: 2, y: 2, z: 4, core: 2. Of those that a mesh axis runs over, the one named last changes fastest.
Arguments:
- picture_tower_vectors: bfloat16 [3072, 1152], P('dp'), may hold values from -6 to 6
- caption_tower_vectors: bfloat16 [3072, 1152], P('dp', 'mp'), may hold values from -6 to 6
- picture_standardize_factor: float32 [1152], replicated, may hold values from 0.1 to 1.9
- picture_entry_matrix: bfloat16 [1152, 4304], P(None, 'mp'), may hold values from -0.1875 to 0.1875
- picture_exit_matrix: bfloat16 [4304, 1152], P('mp'), may hold values from -0.09375 to 0.09375
- caption_mapping_matrix: bfloat16 [1152, 1152], P('mp'), may hold values from -1 to 1
- energy_multiplier: float32 [], replicated, may hold values from 4 to 16
- energy_offset_term: float32 [], replicated, may hold values from -2 to -0.5
Outputs:
- grad_image: float32 [3072, 1152], P('dp', 'mp')
- grad_text: float32 [3072, 1152], P('dp', 'mp')
All inputs are finite; a program needn't handle non-finite values.
Results may differ from a plain program's by a relative error of at most 0.0046.
Values may be sent and summed in bfloat16 or wider, within the bound.
A program may use at most 64 MiB of HBM per device.

v0:
```python
import jax
import jax.numpy as jnp
from jax import lax
from jax.sharding import PartitionSpec as P


def gelu_tanh(values):
    return jax.nn.gelu(values, approximate=True)


def norm_back(upstream, unit_rows, inverse):
    unit_float = unit_rows.astype(jnp.float32)
    along = jnp.sum(unit_float * upstream, axis=-1, keepdims=True)
    return inverse * (upstream - unit_float * along)


def per_device(
    picture_tower_vectors,
    caption_tower_vectors,
    picture_standardize_factor,
    picture_entry_matrix,
    picture_exit_matrix,
    caption_mapping_matrix,
    energy_multiplier,
    energy_offset_term,
):
    rows_here = picture_tower_vectors.shape[0]
    width = picture_tower_vectors.shape[1]
    head_count = lax.axis_size("mp")
    head_pos = lax.axis_index("mp")
    cycle_size = lax.axis_size("dp")
    cycle_pos = lax.axis_index("dp")
    share = rows_here // head_count
    cols_here = caption_tower_vectors.shape[1]
    image_float = picture_tower_vectors.astype(jnp.float32)
    mean_row = jnp.mean(image_float, axis=-1, keepdims=True)
    variance = jnp.mean((image_float - mean_row) ** 2, axis=-1, keepdims=True)
    inv_std = lax.rsqrt(variance + 1e-06)
    centred = (image_float - mean_row) * inv_std
    normed = (centred * picture_standardize_factor).astype(jnp.bfloat16)
    preact = jnp.dot(normed, picture_entry_matrix, preferred_element_type=jnp.float32)
    hidden = gelu_tanh(preact).astype(jnp.bfloat16)
    partial_out = jnp.dot(hidden, picture_exit_matrix, preferred_element_type=jnp.float32)
    image_out = image_float + lax.psum(partial_out, "mp")
    inv_image = lax.rsqrt(jnp.sum(image_out * image_out, axis=-1, keepdims=True) + 1e-06)
    unit_image = (image_out * inv_image).astype(jnp.bfloat16)
    text_out = lax.psum_scatter(
        jnp.dot(caption_tower_vectors, caption_mapping_matrix, preferred_element_type=jnp.float32),
        "mp",
        scatter_dimension=0,
        tiled=True,
    )
    inv_text = lax.rsqrt(jnp.sum(text_out * text_out, axis=-1, keepdims=True) + 1e-06)
    unit_text = (text_out * inv_text).astype(jnp.bfloat16)
    image_ids = cycle_pos * rows_here + jnp.arange(rows_here, dtype=jnp.int32)
    piece = lax.all_gather(unit_text, "dp", axis=0, tiled=True)
    count = piece.shape[0]
    whole_pos = jnp.arange(count, dtype=jnp.int32)
    text_ids = whole_pos // share * rows_here + head_pos * share + whole_pos % share
    cosine_matrix = lax.dot_general(
        piece, unit_image, (((1,), (1,)), ((), ())), preferred_element_type=jnp.float32
    )
    couple_energies = energy_multiplier * cosine_matrix + energy_offset_term
    match_polarity = jnp.where(text_ids[:, None] == image_ids[None, :], 1.0, -1.0).astype(
        jnp.float32
    )
    polarity_scaled_energies = (
        energy_multiplier * -match_polarity * jax.nn.sigmoid(-match_polarity * couple_energies)
    ).astype(jnp.bfloat16)
    image_add = lax.dot_general(
        polarity_scaled_energies,
        piece,
        (((0,), (0,)), ((), ())),
        preferred_element_type=jnp.float32,
    )
    text_add = jnp.dot(polarity_scaled_energies, unit_image, preferred_element_type=jnp.float32)
    image_add, text_add = (image_add, text_add)
    text_store = text_add
    image_dir, text_store = (image_add, text_store)
    returned = lax.all_to_all(text_store, "dp", split_axis=0, concat_axis=0, tiled=True)
    text_dir = jnp.sum(returned.reshape(cycle_size, share, width), axis=0)
    image_total = lax.psum(image_dir, "mp")
    grad_out = norm_back(image_total, unit_image, inv_image)
    grad_out_b = grad_out.astype(jnp.bfloat16)
    grad_hidden = lax.dot_general(
        grad_out_b,
        picture_exit_matrix,
        (((1,), (1,)), ((), ())),
        preferred_element_type=jnp.float32,
    )
    unused, pull_back = jax.vjp(gelu_tanh, preact)
    grad_pre = pull_back(grad_hidden)[0].astype(jnp.bfloat16)
    partial_normed = lax.dot_general(
        grad_pre, picture_entry_matrix, (((1,), (1,)), ((), ())), preferred_element_type=jnp.float32
    )
    grad_normed = lax.psum_scatter(partial_normed, "mp", scatter_dimension=1, tiled=True)
    first_col = head_pos * cols_here
    gain_here = lax.dynamic_slice_in_dim(picture_standardize_factor, first_col, cols_here, 0)
    centred_here = lax.dynamic_slice_in_dim(centred, first_col, cols_here, 1)
    grad_out_here = lax.dynamic_slice_in_dim(grad_out, first_col, cols_here, 1)
    scaled = grad_normed * gain_here
    sum_one, sum_two = lax.psum(
        (jnp.sum(scaled, axis=-1), jnp.sum(scaled * centred_here, axis=-1)), "mp"
    )
    mean_one = (sum_one / width)[:, None]
    mean_two = (sum_two / width)[:, None]
    grad_image = grad_out_here + inv_std * (scaled - mean_one - centred_here * mean_two)
    grad_text_out = norm_back(text_dir, unit_text, inv_text).astype(jnp.bfloat16)
    grad_text = lax.dot_general(
        lax.all_gather(grad_text_out, "mp", axis=0, tiled=True),
        caption_mapping_matrix,
        (((1,), (1,)), ((), ())),
        preferred_element_type=jnp.float32,
    )
    return (grad_image, grad_text)


def solution(mesh):
    in_specs = (
        P("dp", None),
        P("dp", "mp"),
        P(),
        P(None, "mp"),
        P("mp", None),
        P("mp", None),
        P(),
        P(),
    )
    out_specs = (P("dp", "mp"), P("dp", "mp"))
    return jax.shard_map(
        per_device, mesh=mesh, in_specs=in_specs, out_specs=out_specs, check_vma=False
    )
```

profile of v0, /device:TPU:12, one launch (start us, length us, event | category | flops | bytes accessed | tf_op | source)
XLA Modules:
  0.0 306.5 jit_solution(9070903717060754251)
XLA Ops:
  7.2 0.0 copy-start
  7.2 0.0 reduce-scatter.5.cloned.1.call-start
  7.2 1.2 copy-done
  8.5 2.4 fusion.66
  10.9 0.0 reduce-scatter.5.cloned.1.call-update
  10.9 0.0 all-reduce.4.cloned.1.call-start
  11.0 0.1 convert_reduce_fusion
  11.1 0.0 slice-start
  11.2 0.3 fusion.17
  11.4 0.0 slice-start.1
  11.4 4.4 %fusion.37 = f32[192,2152]{1,0:T(8,128)S(1)} fusion(bf16[1152,2152]{0,1:T(8,128)(2,1)} %param.11, f32[1152]{0:T(1024)S(1)} %copy-done.6, bf16[192,1152]{1,0:T(8,128)(2,1)S(1)} %copy-done.2, f32[192]{0:T(256)S(1)} %add_rsqrt_fusion.1, f32[192]{0:T(256)S(1)} %broadcast_multiply_fusion.2), kind=kOutput, calls=%fused_computation.53 | convolution fusion | flops 953081856 | bytes 7059456 | tf_op jit(solution)/shard_map/dot_general | solution.py:41
  15.8 1.2 copy-done.7
  17.0 2.4 fusion.21
  19.4 0.0 all-reduce.4.cloned.1.call-update
  19.4 0.0 all-gather.2.cloned.1.call-start
  19.5 11.3 %reduce-scatter.5.cloned.1.call-done = f32[96,1152]{1,0:T(8,128)} async-done(((f32[192,1152]{1,0:T(8,128)}), f32[96,1152]{1,0:T(8,128)}) %reduce-scatter.5.cloned.1.call-update) | async-done | bytes 442384 | tf_op jit(solution)/shard_map/reduce_scatter | solution.py:47
  30.8 1.1 multiply_reduce_fusion.2
  31.9 1.8 multiply_convert_fusion.5
  33.7 0.0 all-gather.2.cloned.1.call-update
  35.1 34.5 %all-reduce.4.cloned.1.call-done = f32[192,1152]{1,0:T(8,128)} async-done(((f32[192,1152]{1,0:T(8,128)}), f32[192,1152]{1,0:T(8,128)}) %all-reduce.4.cloned.1.call-update) | async-done | bytes 884752 | tf_op jit(solution)/shard_map/psum | solution.py:44
  69.6 1.4 multiply_reduce_fusion
  71.1 0.3 fusion.15
  71.4 47.5 %all-gather.2.cloned.1.call-done = bf16[1536,1152]{1,0:T(8,128)(2,1)} async-done(((bf16[96,1152]{1,0:T(8,128)(2,1)}), bf16[1536,1152]{1,0:T(8,128)(2,1)}) %all-gather.2.cloned.1.call-update) | async-done | bytes 3538960 | tf_op jit(solution)/shard_map/all_gather | solution.py:56
  118.9 3.5 %fusion.7 = bf16[1536,192]{0,1:T(8,128)(2,1)S(1)} fusion(bf16[1536,1152]{1,0:T(8,128)(2,1)} %all-gather.2.cloned.1.call-done, bf16[192,1152]{1,0:T(8,128)(2,1)S(1)} %get-tuple-element.7, f32[]{:T(128)S(6)} %copy.15, s32[1536]{0:T(1024)S(1)} %fusion.53, f32[]{:T(128)S(6)} %copy.14, s32[192]{0:T(256)S(1)} %iota_add_fusion), kind=kOutput, calls=%fused_computation.9 | convolution fusion | flops 683016192 | bytes 4578056 | tf_op jit(solution)/shard_map/dot_general | solution.py:60
  122.4 4.2 %fusion.68 = f32[1536,1152]{1,0:T(8,128)} fusion(bf16[1536,192]{0,1:T(8,128)(2,1)S(1)} %fusion.7, bf16[192,1152]{1,0:T(8,128)(2,1)S(1)} %get-tuple-element.7), kind=kOutput, calls=%fused_computation.93 | convolution fusion | flops 679477248 | bytes 8110080 | tf_op jit(solution)/shard_map/dot_general | solution.py:76
  126.6 5.7 %all-to-all-start = ((f32[16,96,1152]{2,1,0:T(8,128)}), f32[16,96,1152]{2,1,0:T(8,128)}, u32[]{:S(2)}, u32[]{:S(2)}) async-start(f32[16,96,1152]{2,1,0:T(8,128)} %bitcast.18), calls=%async_computation.1 | async-start | bytes 14155776 | tf_op jit(solution)/shard_map/all_to_all | solution.py:80
  132.4 0.0 all-reduce.6.cloned.1.call-start
  132.4 4.1 %fusion.67 = f32[192,1152]{1,0:T(8,128)} fusion(bf16[1536,192]{0,1:T(8,128)(2,1)} %copy-done.3, bf16[1536,1152]{1,0:T(8,128)(2,1)} %all-gather.2.cloned.1.call-done), kind=kOutput, calls=%fused_computation.92 | convolution fusion | flops 679477248 | bytes 5013504 | tf_op jit(solution)/shard_map/dot_general | solution.py:70
  136.5 0.0 all-reduce.6.cloned.1.call-update
  136.5 0.0 reduce-scatter.7.cloned.1.call-start
  136.5 37.5 %all-reduce.6.cloned.1.call-done = f32[192,1152]{1,0:T(8,128)} async-done(((f32[192,1152]{1,0:T(8,128)}), f32[192,1152]{1,0:T(8,128)}) %all-reduce.6.cloned.1.call-update) | async-done | bytes 884752 | tf_op jit(solution)/shard_map/psum | solution.py:82
  174.1 1.4 fusion.18
  175.5 0.0 copy-done.4
  175.5 1.2 fusion.20
  176.7 9.4 %convolution_bitcast_fusion = f32[1152,192]{1,0:T(8,128)} fusion(bf16[1152,2152]{0,1:T(8,128)(2,1)} %param.11, f32[192,2152]{1,0:T(8,128)} %copy-done.7, bf16[2152,1152]{1,0:T(8,128)(2,1)} %param.12, f32[192,1152]{1,0:T(8,128)} %fusion.20), kind=kOutput, calls=%fused_computation | convolution fusion | flops 1912436736 | bytes 13338624
  186.0 0.0 reduce-scatter.7.cloned.1.call-update
  186.1 0.1 dynamic_slice.10
  186.2 21.9 %reduce-scatter.7.cloned.1.call-done = f32[576,192]{1,0:T(8,128)} async-done(((f32[1152,192]{1,0:T(8,128)}), f32[576,192]{1,0:T(8,128)}) %reduce-scatter.7.cloned.1.call-update) | async-done | bytes 442384
  208.1 1.3 copy.11
  209.3 0.3 multiply_reduce_fusion.3
  209.7 4.9 %all-reduce = (f32[192]{0:T(256)S(1)}, f32[192]{0:T(256)S(1)}) all-reduce(f32[192]{0:T(256)S(1)} %get-tuple-element.3, f32[192]{0:T(256)S(1)} %get-tuple-element.2), channel_id=1, replica_groups=mesh['dp'=16,'mp'=2] {'mp'}, use_global_device_ids=true, to_apply=%region_12.13 | all-reduce | flops 384 | bytes 3072 | tf_op jit(solution)/shard_map/psum | solution.py:102
  214.6 2.3 multiply_add_fusion
  216.9 69.5 %all-to-all-done = f32[16,96,1152]{2,1,0:T(8,128)} async-done(((f32[16,96,1152]{2,1,0:T(8,128)}), f32[16,96,1152]{2,1,0:T(8,128)}, u32[]{:S(2)}, u32[]{:S(2)}) %all-to-all-start) | async-done | bytes 7077920 | tf_op jit(solution)/shard_map/all_to_all | solution.py:80
  286.4 3.4 %reduce_sum.88 = f32[96,1152]{1,0:T(8,128)S(1)} reduce(f32[16,96,1152]{2,1,0:T(8,128)} %all-to-all-done, f32[]{:T(128)} %constant.19.clone.1), dimensions={0}, to_apply=%region_13.14 | reduce | flops 1658880 | bytes 7520260 | tf_op jit(solution)/shard_map/reduce_sum | solution.py:81
  289.8 0.2 fusion.33
  290.0 0.1 fusion.36
  290.1 8.4 %all_gather.7 = bf16[192,1152]{1,0:T(8,128)(2,1)S(1)} all-gather(bf16[96,1152]{1,0:T(8,128)(2,1)S(1)} %fusion.36), channel_id=1, replica_groups=mesh['dp'=16,'mp'=2] {'mp'}, dimensions={0}, use_global_device_ids=true | all-gather | bytes 663552 | tf_op jit(solution)/shard_map/all_gather | solution.py:110
  298.5 1.4 fusion.69
  (22 shorter events, 0.1 us)
Async XLA Ops:
  7.2 1.3 copy-start
  7.2 3.8 %copy-start.2 = (bf16[192,1152]{1,0:T(8,128)(2,1)S(1)}, bf16[192,1152]{1,0:T(8,128)(2,1)}, u32[]{:S(2)}) copy-start(bf16[192,1152]{1,0:T(8,128)(2,1)} %param.8) | copy-start | bytes 1327108
  7.2 4.2 %copy-start.6 = (f32[1152]{0:T(1024)S(1)}, f32[1152]{0:T(1024)}, u32[]{:S(2)}) copy-start(f32[1152]{0:T(1024)} %param.10) | copy-start | bytes 13828
  7.2 23.6 %reduce-scatter.5.cloned.1.call-start = ((), (), s32[]{:S(2)}) async-start(), calls=%async_computation.4 | async-start | bytes 1327104 | tf_op jit(solution)/shard_map/reduce_scatter | solution.py:47
  10.9 58.7 %all-reduce.4.cloned.1.call-start = ((), (), s32[]{:S(2)}) async-start(), calls=%async_computation.3 | async-start | bytes 1769472 | tf_op jit(solution)/shard_map/psum | solution.py:44
  11.1 5.9 %slice-start = ((s8[4958208]{0:T(1024)(128)(4,1)}), s8[4194304]{0:T(1024)(128)(4,1)S(1)}, s32[]{:S(2)}) async-start(s8[4958208]{0:T(1024)(128)(4,1)} %bitcast.20), calls=%async_computation.8 | async-start | bytes 8388608
  11.4 5.6 %slice-start.1 = ((s8[4958208]{0:T(1024)(128)(4,1)}), s8[763904]{0:T(1024)(128)(4,1)S(1)}, s32[]{:S(2)}) async-start(s8[4958208]{0:T(1024)(128)(4,1)} %bitcast.20), calls=%async_computation.9 | async-start | bytes 1527808
  15.8 1.2 copy-start.7
  19.4 99.5 %all-gather.2.cloned.1.call-start = ((), (), s32[]{:S(2)}) async-start(), calls=%async_computation.5 | async-start | bytes 3760128 | tf_op jit(solution)/shard_map/all_gather | solution.py:56
  69.6 1.5 copy-start.5
  122.4 4.2 %copy-start.3 = (bf16[1536,192]{0,1:T(8,128)(2,1)}, bf16[1536,192]{0,1:T(8,128)(2,1)S(1)}, u32[]{:S(2)}) copy-start(bf16[1536,192]{0,1:T(8,128)(2,1)S(1)} %fusion.7) | copy-start | bytes 1769476
  126.6 159.7 %all-to-all-start = ((f32[16,96,1152]{2,1,0:T(8,128)}), f32[16,96,1152]{2,1,0:T(8,128)}, u32[]{:S(2)}, u32[]{:S(2)}) async-start(f32[16,96,1152]{2,1,0:T(8,128)} %bitcast.18), calls=%async_computation.1 | async-start | bytes 14155776 | tf_op jit(solution)/shard_map/all_to_all | solution.py:80
  132.4 41.7 %all-reduce.6.cloned.1.call-start = ((), (), s32[]{:S(2)}) async-start(), calls=%async_computation.6 | async-start | bytes 1769472 | tf_op jit(solution)/shard_map/psum | solution.py:82
  136.5 71.6 %reduce-scatter.7.cloned.1.call-start = ((), (), s32[]{:S(2)}) async-start(), calls=%async_computation.7 | async-start | bytes 1769472
  174.1 1.4 copy-start.4
  216.9 72.9 %copy-start.1 = (f32[96,1152]{1,0:T(8,128)S(1)}, f32[96,1152]{1,0:T(8,128)}, u32[]{:S(2)}) copy-start(f32[96,1152]{1,0:T(8,128)} %reduce-scatter.5.cloned.1.call-done) | copy-start | bytes 1327108
Sparse Core Ops, SparseCore 0:
  11.1 19.6 reduce-scatter.4
  33.1 36.4 all-reduce.3
  72.5 46.3 all-gather.1
  136.6 37.4 all-reduce.5
  186.2 21.8 reduce-scatter.6
where the time goes:
time: 307 us; the launch traced here: 306 us
  waiting for transfers between devices  222 us (72%)
  matrix products  31.7 us (10%)
  between operations  15.3 us (5%)
  other arithmetic  14.1 us (5%)
  blocking collectives  13.3 us (4%)
  starting transfers between devices  5.93 us (2%)
  local copies, waits for them, and re-layouts  3.86 us (1%)
    all_to_all x1, waiting for transfers between devices, per_device(): lax.all_to_all(text_store, 'dp', split_axis=0, concat_axis=0, tiled=True)  69.5 us
    all_gather x1, waiting for transfers between devices, per_device(): piece = lax.all_gather(unit_text, 'dp', axis=0, tiled=True)  47.5 us
    psum x1, waiting for transfers between devices, per_device(): image_total = lax.psum(image_dir, 'mp')  37.5 us
    psum x1, waiting for transfers between devices, per_device(): image_out = image_float + lax.psum(partial_out, 'mp')  34.5 us
    unnamed x6, waiting for transfers between devices  22 us
    reduce_scatter x1, waiting for transfers between devices, per_device(): lax.psum_scatter(jnp.dot(caption_tower_vectors, caption_mapping_matrix, p...  11.3 us
    unnamed x1, matrix products  9.36 us
    all_gather x1, blocking collectives, per_device(): lax.all_gather(grad_text_out, 'mp', axis=0, tiled=True)  8.39 us
  transfers between devices with their start and end apart: 6, of which 6 were waited for; matrix products, arithmetic and copies ran while one was open for 10% of the time, Pallas kernels for 0%

commit v1 on v0

v1 whole, which is shorter than its diff:
```python
import functools
import math

import jax
import jax.numpy as jnp
from jax import lax
from jax.experimental import pallas as pl
from jax.experimental.pallas import tpu as pltpu
from jax.sharding import PartitionSpec as P

F32 = jnp.float32
BF16 = jnp.bfloat16
MESH = pl.DeviceIdType.MESH
TILE = 512
ROOT = math.sqrt(2.0 / math.pi)
NT = (((1,), (1,)), ((), ()))


def dot(a, b):
    return jnp.dot(a, b, preferred_element_type=F32)


def dot_nt(a, b):
    return lax.dot_general(a, b, NT, preferred_element_type=F32)


def gelu_pair(x):
    square = x * x
    t = jnp.tanh(ROOT * (x + 0.044715 * (square * x)))
    half = 0.5 * (1.0 + t)
    slope = half + 0.5 * x * (1.0 - t * t) * (ROOT * (1.0 + 0.134145 * square))
    return x * half, slope


def norm_back(upstream, unit_rows, inverse):
    unit_float = unit_rows.astype(F32)
    along = jnp.sum(unit_float * upstream, axis=-1, keepdims=True)
    return inverse * (upstream - unit_float * along)


def body(
    n,
    heads,
    pic_hbm,
    split_hbm,
    cap_hbm,
    gain_ref,
    gains_ref,
    entry_hbm,
    exit_hbm,
    map_hbm,
    scale_ref,
    shift_ref,
    out_go,
    out_rest,
    out_text,
    pic,
    split,
    cap,
    entry,
    exit_,
    mapping,
    load_sem,
    normed,
    slope,
    acc,
    own_f32,
    parts,
    lands,
    fulls,
    ring_text,
    ring_image,
    norm_own,
    norm_part,
    norm_land,
    sums_part,
    sums_land,
    part_send,
    part_recv,
    full_send,
    full_recv,
    norm_send,
    norm_recv,
    sums_send,
    sums_recv,
    ring_send,
    ring_recv,
):
    rows, width = pic.shape
    share = rows // heads
    hidden = entry.shape[1]
    cols = split.shape[2]
    me = lax.axis_index("dp")
    head = lax.axis_index("mp")
    length = n // 4

    def place(index):
        z = index // 4
        y = (index // 2) % 2
        return 2 * (z * (1 - y) + (2 * length - 1 - z) * y) + index % 2

    def device(position):
        position = (position + n) % n
        chip = position // 2
        y = chip // length
        z = chip * (1 - y) + (2 * length - 1 - chip) * y
        return (z * 2 + y) * 2 + position % 2

    pos = place(me)
    right = device(pos + 1)
    left = device(pos - 1)
    forward = n // 2
    backward = n - 1 - forward

    loads = []
    for at, (src, dst) in enumerate(
        (
            (cap_hbm, cap),
            (map_hbm, mapping),
            (pic_hbm, pic),
            (entry_hbm, entry),
            (exit_hbm, exit_),
            (split_hbm, split),
        )
    ):
        copy = pltpu.make_async_copy(src, dst, load_sem.at[at])
        copy.start()
        loads.append(copy)

    barrier = pltpu.get_barrier_semaphore()
    for neighbour in (left, right):
        pl.semaphore_signal(barrier, inc=1, device_id={"dp": neighbour}, device_id_type=MESH)
    for o in range(1, heads):
        pl.semaphore_signal(
            barrier, inc=1, device_id={"mp": (head + o) % heads}, device_id_type=MESH
        )

    def ring_copy(which, buf, way, step):
        block = device(pos - step if way == 0 else pos + step)
        return pltpu.make_async_remote_copy(
            src_ref=buf.at[block],
            dst_ref=buf.at[block],
            send_sem=ring_send.at[which, way, step],
            recv_sem=ring_recv.at[which, way, step],
            device_id={"dp": right if way == 0 else left},
            device_id_type=MESH,
        )

    def ring_start(which, buf, step):
        if step < forward:
            ring_copy(which, buf, 0, step).start()
        if step < backward:
            ring_copy(which, buf, 1, step).start()

    def ring_next(which, buf, step):
        for way, count in ((0, forward), (1, backward)):
            if step < count:
                block = device(pos - step - 1 if way == 0 else pos + step + 1)
                pltpu.make_async_remote_copy(
                    src_ref=buf.at[block],
                    dst_ref=buf.at[block],
                    send_sem=ring_send.at[which, way, step],
                    recv_sem=ring_recv.at[which, way, step],
                    device_id={"dp": right if way == 0 else left},
                    device_id_type=MESH,
                ).wait_recv()
                if step + 1 < count:
                    ring_copy(which, buf, way, step + 1).start()

    def ring_end(which, buf):
        for way, count in ((0, forward), (1, backward)):
            for step in range(count):
                ring_copy(which, buf, way, step).wait_send()

    def exchange(src, dst, send, recv, spread):
        copies = []
        for o in range(1, heads):
            to = (head + o) % heads
            source = (head + heads - o) % heads
            sent = pltpu.make_async_remote_copy(
                src_ref=src.at[to] if spread else src.at[head],
                dst_ref=dst.at[head],
                send_sem=send.at[o],
                recv_sem=recv.at[o],
                device_id={"mp": to},
                device_id_type=MESH,
            )
            got = pltpu.make_async_remote_copy(
                src_ref=dst.at[source],
                dst_ref=dst.at[source],
                send_sem=send.at[o],
                recv_sem=recv.at[o],
                device_id={"mp": to},
                device_id_type=MESH,
            )
            copies.append((sent, got))
        for sent, got in copies:
            sent.start()
        return copies

    def arrived(copies):
        for sent, got in copies:
            got.wait_recv()

    def finished(copies):
        for sent, got in copies:
            sent.wait_send()

    def scatter_start(which, total):
        for p in range(heads):
            piece = total[p * share : (p + 1) * share]
            own_f32[p] = piece
            parts[which, p] = piece.astype(BF16)
        return exchange(
            parts.at[which], lands.at[which], part_send.at[which], part_recv.at[which], True
        )

    def scatter_sum(which, copies, mine):
        arrived(copies)
        for o in range(1, heads):
            mine = mine + lands[which, (head + heads - o) % heads].astype(F32)
        return mine

    def share_start(which, mine):
        fulls[which, head] = mine
        return exchange(
            fulls.at[which], fulls.at[which], full_send.at[which], full_recv.at[which], False
        )

    def full(which):
        return jnp.concatenate([fulls[which, p] for p in range(heads)], axis=0)

    pending = []

    loads[0].wait()
    loads[1].wait()
    text_part = dot(cap[...], mapping[...])
    pl.semaphore_wait(barrier, 2 + heads - 1)
    text_copies = scatter_start(0, text_part)
    pending.append(text_copies)
    text_mine = own_f32[head]

    loads[2].wait()
    image_float = pic[...].astype(F32)
    mean_row = jnp.mean(image_float, axis=-1, keepdims=True)
    variance = jnp.mean((image_float - mean_row) ** 2, axis=-1, keepdims=True)
    inv_std = lax.rsqrt(variance + 1e-06)
    normed[...] = ((image_float - mean_row) * inv_std * gain_ref[...]).astype(BF16)

    text_out = scatter_sum(0, text_copies, text_mine)
    inv_text = lax.rsqrt(jnp.sum(text_out * text_out, axis=-1, keepdims=True) + 1e-06)
    unit_text = (text_out * inv_text).astype(BF16)
    ring_text[me] = unit_text
    ring_start(0, ring_text, 0)
    text_full = share_start(0, unit_text)
    pending.append(text_full)

    loads[3].wait()
    loads[4].wait()
    tiles = [(first, min(TILE, hidden - first)) for first in range(0, hidden, TILE)]
    text_steps = iter(range(forward))

    def advance(steps, which, buf, count):
        for _ in range(count):
            step = next(steps, None)
            if step is not None:
                ring_next(which, buf, step)

    for at, (first, size) in enumerate(tiles):
        span = slice(first, first + size)
        value, grad = gelu_pair(dot(normed[...], entry[:, span]))
        slope[:, span] = grad
        product = dot(value.astype(BF16), exit_[span, :])
        if at == 0:
            acc[...] = product
        else:
            acc[...] += product
        advance(text_steps, 0, ring_text, 1)
    image_copies = scatter_start(1, acc[...])
    pending.append(image_copies)
    mine = own_f32[head] + pic[pl.ds(pl.multiple_of(head * share, 8), share), :].astype(F32)
    advance(text_steps, 0, ring_text, 1)
    image_out = scatter_sum(1, image_copies, mine)
    inv_image = lax.rsqrt(jnp.sum(image_out * image_out, axis=-1, keepdims=True) + 1e-06)
    unit_image = (image_out * inv_image).astype(BF16)
    ring_image[me] = unit_image
    image_full = share_start(1, unit_image)
    pending.append(image_full)
    ring_start(1, ring_image, 0)
    advance(text_steps, 0, ring_text, forward)
    ring_end(0, ring_text)
    arrived(image_full)
    arrived(text_full)

    scale = scale_ref[0, 0]
    shift = shift_ref[0, 0]
    group = 4 if share % 16 == 0 else 1

    def terms(rows_ref, buf):
        acc[...] = jnp.zeros_like(acc)

        def one(g, carry):
            mine = full(rows_ref)
            if group == 1:
                block = buf[g]
            else:
                block = buf[pl.ds(g * group, group)].reshape(group * share, width)
            energy = scale * dot_nt(mine, block) + shift
            shape = (rows, group * share)
            column = lax.broadcasted_iota(jnp.int32, shape, 1)
            ident = column + (g * (group * rows) + head * share)
            for j in range(1, group):
                ident = ident + jnp.where(column >= j * share, rows - share, 0)
            same = ident == lax.broadcasted_iota(jnp.int32, shape, 0) + me * rows
            weight = scale * jax.nn.sigmoid(jnp.where(same, -energy, energy))
            weight = jnp.where(same, -weight, weight).astype(BF16)
            acc[...] += dot(weight, block)
            return carry

        lax.fori_loop(0, n // group, one, 0)

    image_steps = iter(range(forward))
    terms(1, ring_text)
    dir_copies = scatter_start(2, acc[...])
    pending.append(dir_copies)
    dir_mine = own_f32[head]
    advance(image_steps, 1, ring_image, 2)
    image_dir = scatter_sum(2, dir_copies, dir_mine)
    grad_out = norm_back(image_dir, fulls[1, head], inv_image)
    grad_full = share_start(2, grad_out.astype(BF16))
    pending.append(grad_full)
    advance(image_steps, 1, ring_image, 2)
    arrived(grad_full)
    for p in range(heads):
        out_go[p * share : (p + 1) * share] = fulls[2, p]

    grad_b = full(2)
    for at, (first, size) in enumerate(tiles):
        span = slice(first, first + size)
        grad_pre = (dot_nt(grad_b, exit_[span, :]) * slope[:, span]).astype(BF16)
        for p in range(heads):
            product = dot_nt(grad_pre, entry[p * cols : (p + 1) * cols, span])
            if at == 0:
                norm_own[p] = product
            else:
                norm_own[p] += product
        advance(image_steps, 1, ring_image, 1)
    loads[5].wait()
    one_sum = jnp.zeros((rows, 1), F32)
    two_sum = jnp.zeros((rows, 1), F32)
    for p in range(heads):
        piece = norm_own[p]
        norm_part[p] = piece.astype(BF16)
        scaled = piece * gains_ref[p]
        one_sum += jnp.sum(scaled, axis=-1, keepdims=True)
        centred = (split[p].astype(F32) - mean_row) * inv_std
        two_sum += jnp.sum(scaled * centred, axis=-1, keepdims=True)
    lane = lax.broadcasted_iota(jnp.int32, (rows, 128), 1)
    sums_part[head] = jnp.where(lane == 0, one_sum, two_sum)
    norm_copies = exchange(norm_part, norm_land, norm_send, norm_recv, True)
    sums_copies = exchange(sums_part, sums_land, sums_send, sums_recv, False)
    pending.append(norm_copies)
    pending.append(sums_copies)
    advance(image_steps, 1, ring_image, forward)
    ring_end(1, ring_image)

    terms(0, ring_image)
    dirs_copies = scatter_start(3, acc[...])
    pending.append(dirs_copies)
    dirs_mine = own_f32[head]

    arrived(norm_copies)
    arrived(sums_copies)
    grad_normed = norm_own[head]
    sums = sums_part[head]
    for o in range(1, heads):
        source = (head + heads - o) % heads
        grad_normed = grad_normed + norm_land[source].astype(F32)
        sums = sums + sums_land[source]
    mean_one = sums[:, 0:1] * (1.0 / width)
    mean_two = sums[:, 1:2] * (1.0 / width)
    centred = (split[head].astype(F32) - mean_row) * inv_std
    scaled = grad_normed * gains_ref[head]
    out_rest[...] = inv_std * (scaled - mean_one - centred * mean_two)

    text_dir = scatter_sum(3, dirs_copies, dirs_mine)
    grad_text_out = norm_back(text_dir, fulls[0, head], inv_text).astype(BF16)
    last_full = share_start(3, grad_text_out)
    pending.append(last_full)
    arrived(last_full)
    out_text[...] = dot_nt(full(3), mapping[...])
    for copies in pending:
        finished(copies)


def per_device(pic, cap, gain, entry, exit_, mapping, scale, shift):
    rows, width = pic.shape
    n = lax.axis_size("dp")
    heads = lax.axis_size("mp")
    cols = cap.shape[1]
    share = rows // heads
    hidden = entry.shape[1]
    split = pic.reshape(rows, heads, cols).transpose(1, 0, 2)
    anywhere = pl.BlockSpec(memory_space=pl.ANY)
    vmem = pl.BlockSpec(memory_space=pltpu.VMEM)
    smem = pl.BlockSpec(memory_space=pltpu.SMEM)
    dma = pltpu.SemaphoreType.DMA
    go, rest, text = pl.pallas_call(
        functools.partial(body, n, heads),
        out_shape=(
            jax.ShapeDtypeStruct((rows, width), BF16),
            jax.ShapeDtypeStruct((rows, cols), F32),
            jax.ShapeDtypeStruct((rows, mapping.shape[0]), F32),
        ),
        in_specs=[anywhere, anywhere, anywhere, vmem, vmem, anywhere, anywhere, anywhere, smem, smem],
        out_specs=(vmem, vmem, vmem),
        scratch_shapes=[
            pltpu.VMEM(pic.shape, BF16),
            pltpu.VMEM(split.shape, BF16),
            pltpu.VMEM(cap.shape, BF16),
            pltpu.VMEM(entry.shape, BF16),
            pltpu.VMEM(exit_.shape, BF16),
            pltpu.VMEM(mapping.shape, BF16),
            dma((6,)),
            pltpu.VMEM((rows, width), BF16),
            pltpu.VMEM((rows, hidden), F32),
            pltpu.VMEM((rows, width), F32),
            pltpu.VMEM((heads, share, width), F32),
            pltpu.VMEM((4, heads, share, width), BF16),
            pltpu.VMEM((4, heads, share, width), BF16),
            pltpu.VMEM((4, heads, share, width), BF16),
            pltpu.VMEM((n, share, width), BF16),
            pltpu.VMEM((n, share, width), BF16),
            pltpu.VMEM((heads, rows, cols), F32),
            pltpu.VMEM((heads, rows, cols), BF16),
            pltpu.VMEM((heads, rows, cols), BF16),
            pltpu.VMEM((heads, rows, 128), F32),
            pltpu.VMEM((heads, rows, 128), F32),
            dma((4, heads)),
            dma((4, heads)),
            dma((4, heads)),
            dma((4, heads)),
            dma((heads,)),
            dma((heads,)),
            dma((heads,)),
            dma((heads,)),
            dma((2, 2, n // 2)),
            dma((2, 2, n // 2)),
        ],
        compiler_params=pltpu.CompilerParams(
            collective_id=0, has_side_effects=True, vmem_limit_bytes=60 * 2**20
        ),
        name="contrastive",
    )(
        pic,
        split,
        cap,
        gain.reshape(1, width),
        gain.reshape(heads, 1, cols),
        entry,
        exit_,
        mapping,
        scale.reshape(1, 1),
        shift.reshape(1, 1),
    )
    first = lax.axis_index("mp") * cols
    grad_image = lax.dynamic_slice_in_dim(go, first, cols, 1).astype(F32) + rest
    return grad_image, text


def solution(mesh):
    in_specs = (
        P("dp", None),
        P("dp", "mp"),
        P(),
        P(None, "mp"),
        P("mp", None),
        P("mp", None),
        P(),
        P(),
    )
    out_specs = (P("dp", "mp"), P("dp", "mp"))
    return jax.shard_map(
        per_device, mesh=mesh, in_specs=in_specs, out_specs=out_specs, check_vma=False
    )
```

time: 307 us -> 112 us (0.36)
  the two profiles are of different devices: /device:TPU:12 before, /device:TPU:0 now
where the time goes in v1:
time: 112 us
  Pallas kernels  92.4 us (82%)
  local copies, waits for them, and re-layouts  15.2 us (14%)
  other arithmetic  2.03 us (2%)
  between operations  1.95 us (2%)
    pallas_call x1, Pallas kernels, per_device(): pl.pallas_call(functools.partial(body, n, heads), out_shape=(jax.ShapeDty...  92.4 us
    unnamed x2, local copies, waits for them, and re-layouts  10.2 us
    reshape x2, local copies, waits for them, and re-layouts, per_device(): split = pic.reshape(rows, heads, cols).transpose(1, 0, 2)  2.32 us

profile of v1, /device:TPU:0, one launch (start us, length us, event | category | flops | bytes accessed | tf_op | source)
XLA Modules:
  0.0 111.6 jit_solution(15429069044157968653)
XLA Ops:
  0.6 1.5 %reshape.19 = bf16[192,2,576]{2,1,0:T(2,128)(2,1)S(1)} reshape(bf16[192,1152]{1,0:T(8,128)(2,1)} %pic_hbm.1) | data formatting | bytes 884736 | tf_op jit(solution)/shard_map/reshape | solution.py:403
  2.1 0.8 copy.14
  3.0 1.3 %reshape.20.gain_ref = f32[1,1152]{1,0:T(1,128)} reshape(f32[1152]{0:T(1024)} %param.10) | data formatting | bytes 9216 | tf_op jit(solution)/shard_map/reshape | solution.py:458
  4.2 1.4 %reshape.21.gains_ref = f32[2,1,576]{2,1,0:T(1,128)} reshape(f32[1152]{0:T(1024)} %param.10) | data formatting | bytes 9216 | tf_op jit(solution)/shard_map/reshape | solution.py:459
  5.6 8.4 %copy.12.entry_hbm = bf16[1152,2152]{1,0:T(8,128)(2,1)} copy(bf16[1152,2152]{0,1:T(8,128)(2,1)} %param.11) | data formatting | bytes 9916416 | tf_op args[3]
  15.3 92.4 %contrastive.1 = (bf16[192,1152]{1,0:T(8,128)(2,1)}, f32[192,576]{1,0:T(8,128)}, f32[192,576]{1,0:T(8,128)}) custom-call(bf16[192,1152]{1,0:T(8,128)(2,1)} %pic_hbm.1, bf16[2,192,576]{2,1,0:T(8,128)(2,1)} %bitcast.7, bf16[192,576]{1,0:T(8,128)(2,1)} %cap_hbm.1, f32[1,1152]{1,0:T(1,128)} %reshape.20.gain_ref, f32[2,1,576]{2,1,0:T(1,128)} %reshape.21.gains_ref, ...), custom_call_target="tpu_custom_call" | custom-call | tf_op jit(solution)/shard_map/contrastive/pallas_call | solution.py:408
  107.7 2.0 %convert_add_fusion = f32[192,576]{1,0:T(8,128)} fusion(f32[192,576]{1,0:T(8,128)} %get-tuple-element.6, bf16[192,1152]{1,0:T(8,128)(2,1)} %get-tuple-element.5, s32[]{:T(128)S(6)} %select_n.3), kind=kLoop, calls=%fused_computation.1 | loop fusion | flops 221184 | bytes 1105924 | tf_op jit(solution)/shard_map/add | solution.py:467
  109.7 1.8 %copy.18 = f32[192,576]{1,0:T(8,128)} copy(f32[192,576]{1,0:T(8,128)} %get-tuple-element.11) | data formatting | bytes 884736

commit v2 on v1

--- a/solution.py
+++ b/solution.py
@@ -42,10 +42,8 @@
     n,
     heads,
     pic_hbm,
-    split_hbm,
     cap_hbm,
     gain_ref,
-    gains_ref,
     entry_hbm,
     exit_hbm,
     map_hbm,
@@ -55,7 +53,6 @@
     out_rest,
     out_text,
     pic,
-    split,
     cap,
     entry,
     exit_,
@@ -70,6 +67,8 @@
     fulls,
     ring_text,
     ring_image,
+    gains,
+    centres,
     norm_own,
     norm_part,
     norm_land,
@@ -88,8 +87,8 @@
 ):
     rows, width = pic.shape
     share = rows // heads
-    hidden = entry.shape[1]
-    cols = split.shape[2]
+    hidden = exit_.shape[0]
+    cols = width // heads
     me = lax.axis_index("dp")
     head = lax.axis_index("mp")
     length = n // 4
@@ -120,7 +119,6 @@
             (pic_hbm, pic),
             (entry_hbm, entry),
             (exit_hbm, exit_),
-            (split_hbm, split),
         )
     ):
         copy = pltpu.make_async_copy(src, dst, load_sem.at[at])
@@ -245,7 +243,12 @@
     mean_row = jnp.mean(image_float, axis=-1, keepdims=True)
     variance = jnp.mean((image_float - mean_row) ** 2, axis=-1, keepdims=True)
     inv_std = lax.rsqrt(variance + 1e-06)
-    normed[...] = ((image_float - mean_row) * inv_std * gain_ref[...]).astype(BF16)
+    gain = gain_ref[...].reshape(1, width)
+    centred = (image_float - mean_row) * inv_std
+    normed[...] = (centred * gain).astype(BF16)
+    for p in range(heads):
+        gains[p] = gain[:, p * cols : (p + 1) * cols]
+        centres[p] = centred[:, p * cols : (p + 1) * cols]
 
     text_out = scatter_sum(0, text_copies, text_mine)
     inv_text = lax.rsqrt(jnp.sum(text_out * text_out, axis=-1, keepdims=True) + 1e-06)
@@ -268,18 +271,19 @@
 
     for at, (first, size) in enumerate(tiles):
         span = slice(first, first + size)
-        value, grad = gelu_pair(dot(normed[...], entry[:, span]))
+        value, grad = gelu_pair(dot_nt(normed[...], entry[span, :]))
         slope[:, span] = grad
         product = dot(value.astype(BF16), exit_[span, :])
         if at == 0:
             acc[...] = product
         else:
             acc[...] += product
-        advance(text_steps, 0, ring_text, 1)
+        if at % 2 == 1:
+            advance(text_steps, 0, ring_text, 1)
     image_copies = scatter_start(1, acc[...])
     pending.append(image_copies)
     mine = own_f32[head] + pic[pl.ds(pl.multiple_of(head * share, 8), share), :].astype(F32)
-    advance(text_steps, 0, ring_text, 1)
+    advance(text_steps, 0, ring_text, 2)
     image_out = scatter_sum(1, image_copies, mine)
     inv_image = lax.rsqrt(jnp.sum(image_out * image_out, axis=-1, keepdims=True) + 1e-06)
     unit_image = (image_out * inv_image).astype(BF16)
@@ -324,50 +328,51 @@
     dir_copies = scatter_start(2, acc[...])
     pending.append(dir_copies)
     dir_mine = own_f32[head]
-    advance(image_steps, 1, ring_image, 2)
+    advance(image_steps, 1, ring_image, 4)
     image_dir = scatter_sum(2, dir_copies, dir_mine)
     grad_out = norm_back(image_dir, fulls[1, head], inv_image)
     grad_full = share_start(2, grad_out.astype(BF16))
     pending.append(grad_full)
-    advance(image_steps, 1, ring_image, 2)
+    advance(image_steps, 1, ring_image, forward)
+    ring_end(1, ring_image)
+
+    terms(0, ring_image)
+    dirs_copies = scatter_start(3, acc[...])
+    pending.append(dirs_copies)
+    dirs_mine = own_f32[head]
+
     arrived(grad_full)
     for p in range(heads):
         out_go[p * share : (p + 1) * share] = fulls[2, p]
-
     grad_b = full(2)
     for at, (first, size) in enumerate(tiles):
         span = slice(first, first + size)
         grad_pre = (dot_nt(grad_b, exit_[span, :]) * slope[:, span]).astype(BF16)
-        for p in range(heads):
-            product = dot_nt(grad_pre, entry[p * cols : (p + 1) * cols, span])
-            if at == 0:
-                norm_own[p] = product
-            else:
-                norm_own[p] += product
-        advance(image_steps, 1, ring_image, 1)
-    loads[5].wait()
-    one_sum = jnp.zeros((rows, 1), F32)
-    two_sum = jnp.zeros((rows, 1), F32)
+        product = dot(grad_pre, entry[span, :])
+        if at == 0:
+            acc[...] = product
+        else:
+            acc[...] += product
+    total = acc[...]
     for p in range(heads):
-        piece = norm_own[p]
+        piece = total[:, p * cols : (p + 1) * cols]
+        norm_own[p] = piece
         norm_part[p] = piece.astype(BF16)
-        scaled = piece * gains_ref[p]
-        one_sum += jnp.sum(scaled, axis=-1, keepdims=True)
-        centred = (split[p].astype(F32) - mean_row) * inv_std
-        two_sum += jnp.sum(scaled * centred, axis=-1, keepdims=True)
+    norm_copies = exchange(norm_part, norm_land, norm_send, norm_recv, True)
+    scaled = total * gain_ref[...].reshape(1, width)
+    one_sum = jnp.sum(scaled, axis=-1, keepdims=True)
+    centred = (pic[...].astype(F32) - mean_row) * inv_std
+    two_sum = jnp.sum(scaled * centred, axis=-1, keepdims=True)
     lane = lax.broadcasted_iota(jnp.int32, (rows, 128), 1)
     sums_part[head] = jnp.where(lane == 0, one_sum, two_sum)
-    norm_copies = exchange(norm_part, norm_land, norm_send, norm_recv, True)
     sums_copies = exchange(sums_part, sums_land, sums_send, sums_recv, False)
     pending.append(norm_copies)
     pending.append(sums_copies)
-    advance(image_steps, 1, ring_image, forward)
-    ring_end(1, ring_image)
-
-    terms(0, ring_image)
-    dirs_copies = scatter_start(3, acc[...])
-    pending.append(dirs_copies)
-    dirs_mine = own_f32[head]
+
+    text_dir = scatter_sum(3, dirs_copies, dirs_mine)
+    grad_text_out = norm_back(text_dir, fulls[0, head], inv_text).astype(BF16)
+    last_full = share_start(3, grad_text_out)
+    pending.append(last_full)
 
     arrived(norm_copies)
     arrived(sums_copies)
@@ -379,14 +384,10 @@
         sums = sums + sums_land[source]
     mean_one = sums[:, 0:1] * (1.0 / width)
     mean_two = sums[:, 1:2] * (1.0 / width)
-    centred = (split[head].astype(F32) - mean_row) * inv_std
-    scaled = grad_normed * gains_ref[head]
+    centred = centres[head]
+    scaled = grad_normed * gains[head]
     out_rest[...] = inv_std * (scaled - mean_one - centred * mean_two)
 
-    text_dir = scatter_sum(3, dirs_copies, dirs_mine)
-    grad_text_out = norm_back(text_dir, fulls[0, head], inv_text).astype(BF16)
-    last_full = share_start(3, grad_text_out)
-    pending.append(last_full)
     arrived(last_full)
     out_text[...] = dot_nt(full(3), mapping[...])
     for copies in pending:
@@ -400,7 +401,7 @@
     cols = cap.shape[1]
     share = rows // heads
     hidden = entry.shape[1]
-    split = pic.reshape(rows, heads, cols).transpose(1, 0, 2)
+    flipped = entry.T
     anywhere = pl.BlockSpec(memory_space=pl.ANY)
     vmem = pl.BlockSpec(memory_space=pltpu.VMEM)
     smem = pl.BlockSpec(memory_space=pltpu.SMEM)
@@ -412,16 +413,15 @@
             jax.ShapeDtypeStruct((rows, cols), F32),
             jax.ShapeDtypeStruct((rows, mapping.shape[0]), F32),
         ),
-        in_specs=[anywhere, anywhere, anywhere, vmem, vmem, anywhere, anywhere, anywhere, smem, smem],
+        in_specs=[anywhere, anywhere, vmem, anywhere, anywhere, anywhere, smem, smem],
         out_specs=(vmem, vmem, vmem),
         scratch_shapes=[
             pltpu.VMEM(pic.shape, BF16),
-            pltpu.VMEM(split.shape, BF16),
             pltpu.VMEM(cap.shape, BF16),
-            pltpu.VMEM(entry.shape, BF16),
+            pltpu.VMEM(flipped.shape, BF16),
             pltpu.VMEM(exit_.shape, BF16),
             pltpu.VMEM(mapping.shape, BF16),
-            dma((6,)),
+            dma((5,)),
             pltpu.VMEM((rows, width), BF16),
             pltpu.VMEM((rows, hidden), F32),
             pltpu.VMEM((rows, width), F32),
@@ -431,6 +431,8 @@
             pltpu.VMEM((4, heads, share, width), BF16),
             pltpu.VMEM((n, share, width), BF16),
             pltpu.VMEM((n, share, width), BF16),
+            pltpu.VMEM((heads, 1, cols), F32),
+            pltpu.VMEM((heads, rows, cols), F32),
             pltpu.VMEM((heads, rows, cols), F32),
             pltpu.VMEM((heads, rows, cols), BF16),
             pltpu.VMEM((heads, rows, cols), BF16),
@@ -453,11 +455,9 @@
         name="contrastive",
     )(
         pic,
-        split,
         cap,
-        gain.reshape(1, width),
-        gain.reshape(heads, 1, cols),
-        entry,
+        gain,
+        flipped,
         exit_,
         mapping,
         scale.reshape(1, 1),

time: 112 us -> 96.9 us (0.87)
  local copies, waits for them, and re-layouts: 15.2 us -> 1.84 us
  Pallas kernels: 92.4 us -> 90.9 us
    unnamed x2 -> x1, local copies, waits for them, and re-layouts: 10.2 us -> 1.84 us
    reshape x4 -> x0, local copies, waits for them, and re-layouts: 4.97 us -> none  [the longest x2 2.32 us: per_device(): split = pic.reshape(rows, heads, cols).transpose(1, 0, 2)]
    pallas_call x1, Pallas kernels: 92.4 us -> 90.9 us  [per_device(): pl.pallas_call(functools.partial(body, n, heads), out_shape=(jax.ShapeDty...]
where the time goes in v2:
time: 96.9 us; the launch traced here: 96.7 us
  Pallas kernels  90.9 us (94%)
  other arithmetic  2.03 us (2%)
  between operations  1.93 us (2%)
  local copies, waits for them, and re-layouts  1.84 us (2%)
    pallas_call x1, Pallas kernels, per_device(): pl.pallas_call(functools.partial(body, n, heads), out_shape=(jax.ShapeDty...  90.9 us
    add x1, other arithmetic, per_device(): grad_image = lax.dynamic_slice_in_dim(go, first, cols, 1).astype(F32) + rest  2.03 us

profile of v2, /device:TPU:0, one launch (start us, length us, event | category | flops | bytes accessed | tf_op | source)
XLA Modules:
  0.0 96.7 jit_solution(15932006575350617341)
XLA Ops:
  1.9 90.9 %contrastive.1 = (bf16[192,1152]{1,0:T(8,128)(2,1)}, f32[192,576]{1,0:T(8,128)}, f32[192,576]{1,0:T(8,128)}) custom-call(bf16[192,1152]{1,0:T(8,128)(2,1)} %pic_hbm.1, bf16[192,576]{1,0:T(8,128)(2,1)} %cap_hbm.1, f32[1152]{0:T(1024)} %gain_ref.1, bf16[2152,1152]{1,0:T(8,128)(2,1)} %bitcast.5, bf16[2152,1152]{1,0:T(8,128)(2,1)} %exit_hbm.1, ...), custom_call_target="tpu_custom_call" | custom-call | tf_op jit(solution)/shard_map/contrastive/pallas_call | solution.py:409
  92.8 2.0 %convert_add_fusion = f32[192,576]{1,0:T(8,128)} fusion(f32[192,576]{1,0:T(8,128)} %get-tuple-element.6, bf16[192,1152]{1,0:T(8,128)(2,1)} %get-tuple-element.5, s32[]{:T(128)S(6)} %select_n.3), kind=kLoop, calls=%fused_computation | loop fusion | flops 221184 | bytes 1105924 | tf_op jit(solution)/shard_map/add | solution.py:467
  94.9 1.8 %copy.13 = f32[192,576]{1,0:T(8,128)} copy(f32[192,576]{1,0:T(8,128)} %get-tuple-element.11) | data formatting | bytes 884736
